TPU v7x, 128 devices: a whole 4x4x4 slice. The times are simulated.
128 devices in a mesh: ta: 4 (over x), gz: 8 (over y, core), xy: 4 (over z).
Axes of the slice: x: 4, y: 4, z: 4, core: 2. Of those that a mesh axis runs over, the one named last changes fastest.
Arguments:
- source: float32 [2, 4, 3, 16, 64, 512], P(None, None, None, 'ta', 'gz', 'xy'), may hold values from -6 to 6
- iterate: float32 [2, 4, 3, 16, 64, 512], P(None, None, None, 'ta', 'gz', 'xy'), may hold values from -6 to 6
- gauge_links: float32 [4, 2, 3, 3, 16, 64, 512], P(None, None, None, None, 'ta', 'gz', 'xy'), may hold values from -2.4 to 2.4
- clover: float32 [2, 2, 6, 6, 16, 64, 512], P(None, None, None, None, 'ta', 'gz', 'xy'), may hold values from -0.6 to 0.6
- bc_sign: int32 [4], replicated, may hold values from -1 to 1, as said below
- null_store: bfloat16 [4, 16, 4, 2, 24, 12, 4, 4, 128], P('ta', 'gz', 'xy'), may hold values from -0.109375 to 0.109375
- block_slot: int32 [4, 16, 4], P('ta', 'gz', 'xy'), may hold values from 0 to 1, as said below
- coarse_links: float32 [9, 2, 24, 24, 4, 16, 4, 8], P(None, None, None, None, 'ta', 'gz', 'xy'), may hold values from -0.2 to 0.2
Outputs:
- new_iterate: float32 [2, 4, 3, 16, 64, 512], P(None, None, None, 'ta', 'gz', 'xy')
- new_residual: float32 [2, 4, 3, 16, 64, 512], P(None, None, None, 'ta', 'gz', 'xy')
Inputs may be any that keep to these rules, and one draw needn't show every extreme that they name: `bc_sign`: each entry is -1 or +1. `block_slot`: within each device's block of 2 aggregate columns the entries are the numbers 0 to 1, each once.
All inputs are finite; a program needn't handle non-finite values.
Results may differ from a plain program's by a relative error of at most 0.0016.
Values sent between devices are 32-bit elements; how exact they have to be, the bound alone decides.
A program may use at most 256 MiB of HBM per device.

v0:
```python
import jax
import jax.numpy as jnp
from jax import lax
from jax.experimental import pallas as pl
from jax.experimental.pallas import tpu as pltpu
from jax.sharding import PartitionSpec as P

MASS_TERM = 3.8
RELAX_WEIGHT = 0.4
NV = 24
HIGHEST = lax.Precision.HIGHEST
MESH = pl.DeviceIdType.MESH
F32 = jnp.float32

UPPER = (((0, 0), (1, 0)), ((0, 3), (1, 1)), ((1, 3), (0, 3)), ((1, 2), (0, 0)))
LOWER = (((0, 0), (1, 0)), ((0, 1), (1, 3)), ((1, 1), (0, 1)), ((1, 0), (0, 2)))


def plus_phase(a, b, power):
    power = power % 4
    if power == 0:
        return (a[0] + b[0], a[1] + b[1])
    if power == 1:
        return (a[0] - b[1], a[1] + b[0])
    if power == 2:
        return (a[0] - b[0], a[1] - b[1])
    return (a[0] + b[1], a[1] - b[0])


def spin_of(ref, spin, t):
    return (ref[0, spin, :, t], ref[1, spin, :, t])


def project(ref, t, mu, sign):
    turn = 0 if sign > 0 else 2
    return [
        plus_phase(spin_of(ref, s, t), spin_of(ref, 2 + UPPER[mu][s][0], t), UPPER[mu][s][1] + turn)
        for s in range(2)
    ]


def times_link(links, mu, t, half):
    out = [None, None]
    for b in range(3):
        ur = links[mu, 0, :, b, t]
        ui = links[mu, 1, :, b, t]
        for s in range(2):
            br = half[s][0][b][None]
            bi = half[s][1][b][None]
            re = ur * br - ui * bi
            im = ur * bi + ui * br
            out[s] = (re, im) if b == 0 else (out[s][0] + re, out[s][1] + im)
    return out


def times_dagger(links, mu, t, half):
    out = [None, None]
    for b in range(3):
        ur = links[mu, 0, b, :, t]
        ui = links[mu, 1, b, :, t]
        for s in range(2):
            br = half[s][0][b][None]
            bi = half[s][1][b][None]
            re = ur * br + ui * bi
            im = ur * bi - ui * br
            out[s] = (re, im) if b == 0 else (out[s][0] + re, out[s][1] + im)
    return out


def add_hop(total, half, mu, sign):
    turn = 0 if sign > 0 else 2
    if total is None:
        zero = jnp.zeros_like(half[0][0])
        total = [half[0], half[1], (zero, zero), (zero, zero)]
    else:
        total = [
            plus_phase(total[0], half[0], 0),
            plus_phase(total[1], half[1], 0),
            total[2],
            total[3],
        ]
    for s in range(2):
        source, power = LOWER[mu][s]
        total[2 + s] = plus_phase(total[2 + s], half[source], power + turn)
    return total


def each(half, function):
    return [(function(re), function(im)) for re, im in half]


def both(first, second, function):
    return [(function(a[0], b[0]), function(a[1], b[1])) for a, b in zip(first, second)]


def kernel(
    source_h, iterate_h, links_h, clover_h, null_h, coarse_h, bc_ref, slot_ref,
    out_x_h, out_r_h,
    source, iterate, links, clover, null_b, coarse_b, null_f, packed,
    ht, gt, gz, gx, hz_s, gz_s, hx_s, gx_s, hz_r, gz_r, hx_r, gx_r,
    part, res, corr, out_x, out_r, field, racc, rrep, coef, wbuf,
    c_t, c_z, c_x, local_sem, send_sem, recv_sem,
):
    me = (lax.axis_index("ta"), lax.axis_index("gz"), lax.axis_index("xy"))
    size = (lax.axis_size("ta"), lax.axis_size("gz"), lax.axis_size("xy"))

    def peer(axis, step):
        place = list(me)
        place[axis] = lax.rem(me[axis] + step + size[axis], size[axis])
        return tuple(place)

    loads = [
        pltpu.make_async_copy(source_from, into, local_sem.at[i])
        for i, (source_from, into) in enumerate((
            (iterate_h, iterate), (links_h, links), (clover_h, clover), (source_h, source),
            (coarse_h, coarse_b), (null_h, null_b),
        ))
    ]
    for load in loads:
        load.start()
    barrier = pltpu.get_barrier_semaphore()
    for axis in range(3):
        for step in (-1, 1):
            pl.semaphore_signal(barrier, inc=1, device_id=peer(axis, step), device_id_type=MESH)

    lane = lax.broadcasted_iota(jnp.int32, (3, 8, 128), 2)
    row = lax.broadcasted_iota(jnp.int32, (3, 8, 128), 1)
    place_y = lane % 32

    def sign_of(mu, at_edge):
        return jnp.where(at_edge, bc_ref[mu], 1).astype(F32)

    top = [sign_of(axis, me[axis] == size[axis] - 1) for axis in range(3)]
    bottom = [sign_of(axis, me[axis] == 0) for axis in range(3)]
    sign_y = bc_ref[3].astype(F32)

    def remote(phase, d, source_from, into):
        return pltpu.make_async_remote_copy(
            src_ref=source_from, dst_ref=into, send_sem=send_sem.at[phase, d],
            recv_sem=recv_sem.at[phase, d],
            device_id=peer(d // 2, -1 if d % 2 == 0 else 1), device_id_type=MESH,
        )

    def store_half(ref, index, half):
        for s in range(2):
            ref[index + (0, s)] = half[s][0]
            ref[index + (1, s)] = half[s][1]

    def load_half(ref, index):
        return [(ref[index + (0, s)], ref[index + (1, s)]) for s in range(2)]

    def fine_copies(n):
        phase = 4 * n
        return [
            remote(phase, 0, ht.at[n, 0], ht.at[n, 4]),
            remote(phase, 1, gt.at[n, 4], gt.at[n, 0]),
            remote(phase, 2, hz_s.at[n], hz_r.at[n]),
            remote(phase, 3, gz_s.at[n], gz_r.at[n]),
            remote(phase, 4, hx_s.at[n], hx_r.at[n]),
            remote(phase, 5, gx_s.at[n], gx_r.at[n]),
        ]

    def fine_send(vec, n):
        copies = fine_copies(n)

        def step_x(t, carry):
            shift_up = t * 32
            half = project(vec, t, 2, -1)
            here = lane // 32 == t
            old = load_half(hx_s, (n,))
            store_half(hx_s, (n,), both(half, old, lambda a, b: jnp.where(here, pltpu.roll(a, shift_up, 2), b)))
            back = times_dagger(links, 2, t, project(vec, t, 2, 1))
            store_half(gx, (t,), back)
            shift_down = lax.rem(t * 32 + 32, 128)
            old = load_half(gx_s, (n,))
            store_half(gx_s, (n,), both(back, old, lambda a, b: jnp.where(here, pltpu.roll(a, shift_down, 2), b)))
            return carry

        def step_t(t, carry):
            store_half(ht, (n, t), project(vec, t, 0, -1))
            store_half(gt, (n, t + 1), times_dagger(links, 0, t, project(vec, t, 0, 1)))
            return carry

        def step_z(t, carry):
            half = project(vec, t, 1, -1)
            store_half(hz_s, (n, t), each(half, lambda a: a[:, 0:1, :]))
            back = times_dagger(links, 1, t, project(vec, t, 1, 1))
            store_half(gz, (t,), back)
            store_half(gz_s, (n, t), each(back, lambda a: a[:, 7:8, :]))
            return carry

        lax.fori_loop(0, 4, step_x, 0)
        if n == 0:
            pl.semaphore_wait(barrier, 6)
        copies[4].start()
        copies[5].start()
        lax.fori_loop(0, 4, step_t, 0)
        copies[0].start()
        copies[1].start()
        lax.fori_loop(0, 4, step_z, 0)
        copies[2].start()
        copies[3].start()
        return copies

    def fine_inner(start, vec):
        def step(t, carry):
            half = project(vec, t, 3, -1)
            half = each(half, lambda a: jnp.where(place_y == 31, sign_y * pltpu.roll(a, 31, 2), pltpu.roll(a, 127, 2)))
            total = add_hop(None, times_link(links, 3, t, half), 3, -1)
            back = times_dagger(links, 3, t, project(vec, t, 3, 1))
            back = each(back, lambda a: jnp.where(place_y == 0, sign_y * pltpu.roll(a, 97, 2), pltpu.roll(a, 1, 2)))
            total = add_hop(total, back, 3, 1)
            for chirality in range(2):
                out_re = [None, None]
                out_im = [None, None]
                for column in range(6):
                    spin, colour = 2 * chirality + column // 3, column % 3
                    vr = vec[0, spin, colour, t][None]
                    vi = vec[1, spin, colour, t][None]
                    for s in range(2):
                        mr = clover[chirality, 0, 3 * s : 3 * s + 3, column, t]
                        mi = clover[chirality, 1, 3 * s : 3 * s + 3, column, t]
                        re = mr * vr - mi * vi
                        im = mr * vi + mi * vr
                        out_re[s] = re if column == 0 else out_re[s] + re
                        out_im[s] = im if column == 0 else out_im[s] + im
                for s in range(2):
                    spin = 2 * chirality + s
                    vr, vi = spin_of(vec, spin, t)
                    part[0, spin, :, t] = start[0, spin, :, t] - MASS_TERM * vr - out_re[s] + 0.5 * total[spin][0]
                    part[1, spin, :, t] = start[1, spin, :, t] - MASS_TERM * vi - out_im[s] + 0.5 * total[spin][1]
            return carry

        lax.fori_loop(0, 4, step, 0)

    def fine_outer(vec, n, out):
        def step(t, carry):
            ahead = jnp.where(t == 3, top[0], 1.0)
            behind = jnp.where(t == 0, bottom[0], 1.0)
            half = each(load_half(ht, (n, t + 1)), lambda a: a * ahead)
            total = add_hop(None, times_link(links, 0, t, half), 0, -1)
            total = add_hop(total, each(load_half(gt, (n, t)), lambda a: a * behind), 0, 1)
            edge = load_half(hz_r, (n, t))
            half = both(project(vec, t, 1, -1), edge, lambda a, b: jnp.where(row == 7, b * top[1], pltpu.roll(a, 7, 1)))
            total = add_hop(total, times_link(links, 1, t, half), 1, -1)
            edge = load_half(gz_r, (n, t))
            back = both(load_half(gz, (t,)), edge, lambda a, b: jnp.where(row == 0, b * bottom[1], pltpu.roll(a, 1, 1)))
            total = add_hop(total, back, 1, 1)
            shift = 96 - 32 * t
            edge = load_half(hx_r, (n,))
            half = both(
                project(vec, t, 2, -1), edge,
                lambda a, b: jnp.where(lane >= 96, pltpu.roll(b, shift, 2) * top[2], pltpu.roll(a, 96, 2)),
            )
            total = add_hop(total, times_link(links, 2, t, half), 2, -1)
            shift_back = lax.rem(128 - 32 * t, 128)
            edge = load_half(gx_r, (n,))
            back = both(
                load_half(gx, (t,)), edge,
                lambda a, b: jnp.where(lane < 32, pltpu.roll(b, shift_back, 2) * bottom[2], pltpu.roll(a, 32, 2)),
            )
            total = add_hop(total, back, 2, 1)
            for spin in range(4):
                out[0, spin, :, t] = part[0, spin, :, t] + 0.5 * total[spin][0]
                out[1, spin, :, t] = part[1, spin, :, t] + 0.5 * total[spin][1]
            return carry

        lax.fori_loop(0, 4, step, 0)

    loads[0].wait()
    loads[1].wait()
    first = fine_send(iterate, 0)
    loads[2].wait()
    loads[3].wait()
    fine_inner(source, iterate)

    loads[4].wait()
    gap = jnp.zeros((2, 8, 8), F32)

    def pack_step(k, carry):
        for p in range(2):
            for group in range(6):
                pieces = []
                for c in range(4):
                    pieces += [coarse_b[k, p, 4 * group + c], gap]
                packed[k, p, group] = jnp.concatenate(pieces, axis=-1)
        return carry

    lax.fori_loop(0, 9, pack_step, 0)
    loads[5].wait()

    def widen_step(v, carry):
        for k in range(2):
            for p in range(2):
                null_f[k, p, v] = null_b[k, p, v].astype(F32)
        return carry

    lax.fori_loop(0, NV, widen_step, 0)
    rrep[...] = jnp.zeros_like(rrep)
    for copy in first:
        copy.wait_recv()
    fine_outer(iterate, 0, res)

    swapped = slot_ref[0] == 1
    row2 = lax.broadcasted_iota(jnp.int32, (8, 128), 0)
    lane2 = lax.broadcasted_iota(jnp.int32, (8, 128), 1)
    spread = (lane2 % 32 // 4 == row2).astype(F32)

    def turn_step(s, carry):
        spin, colour = s // 3, lax.rem(s, 3)
        for q in range(2):
            for pair in range(2):
                first_t = res[q, spin, colour, 2 * pair].astype(jnp.bfloat16).astype(F32)
                second_t = res[q, spin, colour, 2 * pair + 1].astype(jnp.bfloat16).astype(F32)
                low = jnp.where(row2 < 4, first_t, pltpu.roll(second_t, 4, 0))
                high = jnp.where(row2 < 4, pltpu.roll(first_t, 4, 0), second_t)
                field[0, q, s, pair] = jnp.where(swapped, high, low)
                field[1, q, s, pair] = jnp.where(swapped, low, high)
        return carry

    lax.fori_loop(0, 12, turn_step, 0)

    def restrict_step(i, carry):
        k, v = i // NV, lax.rem(i, NV)
        total_re = [None, None]
        total_im = [None, None]
        for s in range(12):
            for pair in range(2):
                nr = null_f[k, 0, v, s, 8 * pair : 8 * pair + 8]
                ni = null_f[k, 1, v, s, 8 * pair : 8 * pair + 8]
                fr = field[k, 0, s, pair]
                fi = field[k, 1, s, pair]
                re = nr * fr + ni * fi
                im = nr * fi - ni * fr
                total_re[pair] = re if s == 0 else total_re[pair] + re
                total_im[pair] = im if s == 0 else total_im[pair] + im
        racc[k, 0, v] = total_re[0] + total_re[1]
        racc[k, 1, v] = total_im[0] + total_im[1]
        return carry

    lax.fori_loop(0, 2 * NV, restrict_step, 0)
    tiles = []
    for k in range(2):
        for q in range(2):
            summed = jnp.sum(racc[k, q], axis=1)
            for c in range(4):
                rrep[k, q, 32 * c : 32 * c + NV] = summed
            tiles.append(
                lax.dot_general(
                    spread, rrep[k, q], (((1,), (1,)), ((), ())), precision=HIGHEST,
                    preferred_element_type=F32,
                )
            )
    rhs = [
        [jnp.where(swapped, tiles[2 + p], tiles[p]) for p in range(2)],
        [jnp.where(swapped, tiles[p], tiles[2 + p]) for p in range(2)],
    ]

    w = [[RELAX_WEIGHT * rhs[z][p] for p in range(2)] for z in range(2)]
    lane6 = lax.broadcasted_iota(jnp.int32, (6, 8, 128), 2)
    segment = lane2 // 32
    sent = []
    for iteration in range(3):
        for z in range(2):
            for p in range(2):
                wbuf[iteration, z, p] = w[z][p]
        phase = 1 + iteration
        copies = [
            remote(phase, 0, wbuf.at[iteration], c_t.at[iteration, 0]),
            remote(phase, 1, wbuf.at[iteration], c_t.at[iteration, 1]),
            remote(phase, 2, wbuf.at[iteration, 0], c_z.at[iteration, 0]),
            remote(phase, 3, wbuf.at[iteration, 1], c_z.at[iteration, 1]),
            remote(phase, 4, wbuf.at[iteration], c_x.at[iteration, 0]),
            remote(phase, 5, wbuf.at[iteration], c_x.at[iteration, 1]),
        ]
        for copy in copies:
            copy.start()
        sent += copies
        sums = [None, None]

        def accumulate(z, k, vector):
            lr = packed[k, 0, :, z]
            li = packed[k, 1, :, z]
            wr, wi = vector[0][None], vector[1][None]
            re = lr * wr - li * wi
            im = lr * wi + li * wr
            sums[z] = (re, im) if sums[z] is None else (sums[z][0] + re, sums[z][1] + im)

        for z in range(2):
            accumulate(z, 0, w[z])
            accumulate(z, 7, [pltpu.roll(a, 7, 0) for a in w[z]])
            accumulate(z, 8, [pltpu.roll(a, 1, 0) for a in w[z]])
        accumulate(0, 3, w[1])
        accumulate(1, 4, w[0])
        for copy in copies:
            copy.wait_recv()
        for z in range(2):
            for k, ref in ((1, c_t.at[iteration, 0]), (2, c_t.at[iteration, 1]), (5, c_x.at[iteration, 0]), (6, c_x.at[iteration, 1])):
                accumulate(z, k, (ref[z, 0], ref[z, 1]))
        accumulate(1, 3, (c_z[iteration, 0, 0], c_z[iteration, 0, 1]))
        accumulate(0, 4, (c_z[iteration, 1, 0], c_z[iteration, 1, 1]))
        new = []
        for z in range(2):
            row_new = []
            for p in range(2):
                x = sums[z][p]
                for shift in (16, 8, 4, 2, 1):
                    x = x + pltpu.roll(x, 128 - shift, 2)
                row_new.append(jnp.where(lane6 % 32 == 0, x, 0.0))
            new.append(row_new)
        w = [
            [
                w[z][p] + RELAX_WEIGHT * (rhs[z][p] - (2.0 * w[z][p] + gather_lanes(new[z][p], segment)))
                for p in range(2)
            ]
            for z in range(2)
        ]

    for z in range(2):
        for p in range(2):
            chosen = jnp.where(swapped, w[1 - z][p], w[z][p]).astype(jnp.bfloat16).astype(F32)
            coef[z, p] = jnp.dot(
                jnp.transpose(chosen), spread, precision=HIGHEST, preferred_element_type=F32
            )

    def prolong_step(s, carry):
        spin, colour = s // 3, lax.rem(s, 3)
        made = []
        for k in range(2):
            total_re = [None, None]
            total_im = [None, None]
            for v in range(NV):
                cr = coef[k, 0, v : v + 1]
                ci = coef[k, 1, v : v + 1]
                for pair in range(2):
                    nr = null_f[k, 0, v, s, 8 * pair : 8 * pair + 8]
                    ni = null_f[k, 1, v, s, 8 * pair : 8 * pair + 8]
                    re = nr * cr - ni * ci
                    im = nr * ci + ni * cr
                    total_re[pair] = re if v == 0 else total_re[pair] + re
                    total_im[pair] = im if v == 0 else total_im[pair] + im
            made.append((total_re, total_im))
        for q in range(2):
            for pair in range(2):
                low = jnp.where(swapped, made[1][q][pair], made[0][q][pair])
                high = jnp.where(swapped, made[0][q][pair], made[1][q][pair])
                corr[q, spin, colour, 2 * pair] = jnp.where(row2 < 4, low, pltpu.roll(high, 4, 0))
                corr[q, spin, colour, 2 * pair + 1] = jnp.where(row2 < 4, pltpu.roll(low, 4, 0), high)
        return carry

    lax.fori_loop(0, 12, prolong_step, 0)

    second = fine_send(corr, 1)

    def add_step(t, carry):
        out_x[:, :, :, t] = iterate[:, :, :, t] + corr[:, :, :, t]
        return carry

    lax.fori_loop(0, 4, add_step, 0)
    store_x = pltpu.make_async_copy(out_x, out_x_h, local_sem.at[6])
    store_x.start()
    fine_inner(res, corr)
    for copy in second:
        copy.wait_recv()
    fine_outer(corr, 1, out_r)
    store_r = pltpu.make_async_copy(out_r, out_r_h, local_sem.at[7])
    store_r.start()
    for copy in first + sent + second:
        copy.wait_send()
    store_x.wait()
    store_r.wait()


def gather_lanes(x, segment):
    y = x[0]
    for group in range(1, 6):
        y = y + pltpu.roll(x[group], 4 * group, 1)
    placed = y
    for c in range(1, 4):
        placed = jnp.where(segment == c, pltpu.roll(y, c, 1), placed)
    placed = placed + pltpu.roll(placed, 64, 1)
    return placed + pltpu.roll(placed, 32, 1)


def per_device(source, iterate, gauge_links, clover, bc_sign, null_store, block_slot, coarse_links):
    null = null_store.reshape((2, 2, NV, 12, 16, 128))
    coarse = jnp.transpose(coarse_links, (0, 1, 2, 4, 5, 6, 7, 3)).reshape((9, 2, NV, 2, 8, NV))
    slots = block_slot.reshape((2,))
    spinor = jax.ShapeDtypeStruct((2, 4, 3, 4, 8, 128), F32)
    anywhere = pl.BlockSpec(memory_space=pl.ANY)
    scalars = pl.BlockSpec(memory_space=pltpu.SMEM)
    half = (2, 2, 3, 8, 128)
    vmem = lambda *shape: pltpu.VMEM(shape, F32)
    return pl.pallas_call(
        kernel,
        out_shape=(spinor, spinor),
        in_specs=[anywhere] * 6 + [scalars] * 2,
        out_specs=(anywhere, anywhere),
        scratch_shapes=[
            vmem(*spinor.shape), vmem(*spinor.shape), vmem(4, 2, 3, 3, 4, 8, 128),
            vmem(2, 2, 6, 6, 4, 8, 128), pltpu.VMEM((2, 2, NV, 12, 16, 128), jnp.bfloat16),
            vmem(9, 2, NV, 2, 8, NV), vmem(2, 2, NV, 12, 16, 128), vmem(9, 2, 6, 2, 8, 128),
            vmem(2, 5, *half), vmem(2, 5, *half), vmem(4, *half), vmem(4, *half),
            vmem(2, 4, 2, 2, 3, 1, 128), vmem(2, 4, 2, 2, 3, 1, 128), vmem(2, *half), vmem(2, *half),
            vmem(2, 4, 2, 2, 3, 1, 128), vmem(2, 4, 2, 2, 3, 1, 128), vmem(2, *half), vmem(2, *half),
            vmem(*spinor.shape), vmem(*spinor.shape), vmem(*spinor.shape), vmem(*spinor.shape),
            vmem(*spinor.shape), vmem(2, 2, 12, 2, 8, 128), vmem(2, 2, NV, 8, 128),
            vmem(2, 2, 128, 128), vmem(2, 2, 128, 128), vmem(3, 2, 2, 8, 128),
            vmem(3, 2, 2, 2, 8, 128), vmem(3, 2, 2, 8, 128), vmem(3, 2, 2, 2, 8, 128),
            pltpu.SemaphoreType.DMA((8,)), pltpu.SemaphoreType.DMA((5, 6)),
            pltpu.SemaphoreType.DMA((5, 6)),
        ],
        compiler_params=pltpu.CompilerParams(
            collective_id=0, has_side_effects=True, vmem_limit_bytes=60 * 1024 * 1024
        ),
    )(source, iterate, gauge_links, clover, null, coarse, bc_sign, slots)


def solution(mesh):
    spinor = P(None, None, None, "ta", "gz", "xy")
    matrix = P(None, None, None, None, "ta", "gz", "xy")
    column = P("ta", "gz", "xy", None, None, None, None, None, None)
    placed = (
        spinor, spinor, matrix, matrix, P(), column, P("ta", "gz", "xy"),
        P(None, None, None, None, "ta", "gz", "xy", None),
    )
    return jax.shard_map(
        per_device, mesh=mesh, in_specs=placed, out_specs=(spinor, spinor), check_vma=False
    )
```

profile of v0, /device:TPU:1, one launch (start us, length us, event | category | flops | bytes accessed | tf_op | source)
XLA Modules:
  0.0 39.2 jit_solution(7557276075172236117)
XLA Ops:
  0.6 35.1 %shard_map.95 = (f32[2,4,3,4,8,128]{5,4,3,2,1,0:T(8,128)}, f32[2,4,3,4,8,128]{5,4,3,2,1,0:T(8,128)}) custom-call(f32[2,4,3,4,8,128]{5,4,3,2,1,0:T(8,128)} %source_h.1, f32[2,4,3,4,8,128]{5,4,3,2,1,0:T(8,128)} %iterate_h.1, f32[4,2,3,3,4,8,128]{6,5,4,3,2,1,0:T(8,128)} %links_h.1, f32[2,2,6,6,4,8,128]{6,5,4,3,2,1,0:T(8,128)} %clover_h.1, ...), custom_call_target="tpu_custom_call" | custom-call | tf_op jit(solution)/shard_map/pallas_call | solution.py:494
  35.7 1.8 %copy.13 = f32[2,4,3,4,8,128]{5,4,3,2,1,0:T(8,128)} copy(f32[2,4,3,4,8,128]{5,4,3,2,1,0:T(8,128)} %get-tuple-element.4) | data formatting | bytes 786432
  37.5 1.8 %copy.14 = f32[2,4,3,4,8,128]{5,4,3,2,1,0:T(8,128)} copy(f32[2,4,3,4,8,128]{5,4,3,2,1,0:T(8,128)} %get-tuple-element.5) | data formatting | bytes 786432
where the time goes:
time: 39.4 us; the launch traced here: 39.2 us
  Pallas kernels  35.1 us (89%)
  local copies, waits for them, and re-layouts  3.53 us (9%)
  between operations  0.64 us (2%)
    pallas_call x1, Pallas kernels, per_device(): pl.pallas_call(kernel, out_shape=(spinor, spinor), in_specs=[anywhere] *...  35.1 us
    unnamed x2, local copies, waits for them, and re-layouts  3.53 us

commit v1 on v0

--- a/solution.py
+++ b/solution.py
@@ -95,11 +95,11 @@
 
 def kernel(
     source_h, iterate_h, links_h, clover_h, null_h, coarse_h, bc_ref, slot_ref,
-    out_x_h, out_r_h,
-    source, iterate, links, clover, null_b, coarse_b, null_f, packed,
+    out_x, out_r,
+    source, iterate, links, clover, null_b, coarse_b, packed,
     ht, gt, gz, gx, hz_s, gz_s, hx_s, gx_s, hz_r, gz_r, hx_r, gx_r,
-    part, res, corr, out_x, out_r, field, racc, rrep, coef, wbuf,
-    c_t, c_z, c_x, local_sem, send_sem, recv_sem,
+    part, res, corr, wide, field, rrow, coef, tile, wbuf,
+    c_halo, local_sem, send_sem, recv_sem,
 ):
     me = (lax.axis_index("ta"), lax.axis_index("gz"), lax.axis_index("xy"))
     size = (lax.axis_size("ta"), lax.axis_size("gz"), lax.axis_size("xy"))
@@ -177,7 +177,7 @@
             return carry
 
         def step_t(t, carry):
-            store_half(ht, (n, t), project(vec, t, 0, -1))
+            store_half(ht, (n, t + 1), project(vec, t + 1, 0, -1))
             store_half(gt, (n, t + 1), times_dagger(links, 0, t, project(vec, t, 0, 1)))
             return carry
 
@@ -189,17 +189,19 @@
             store_half(gz_s, (n, t), each(back, lambda a: a[:, 7:8, :]))
             return carry
 
-        lax.fori_loop(0, 4, step_x, 0)
+        store_half(ht, (n, 0), project(vec, 0, 0, -1))
+        store_half(gt, (n, 4), times_dagger(links, 0, 3, project(vec, 3, 0, 1)))
         if n == 0:
             pl.semaphore_wait(barrier, 6)
+        copies[0].start()
+        copies[1].start()
+        lax.fori_loop(0, 4, step_x, 0)
         copies[4].start()
         copies[5].start()
-        lax.fori_loop(0, 4, step_t, 0)
-        copies[0].start()
-        copies[1].start()
         lax.fori_loop(0, 4, step_z, 0)
         copies[2].start()
         copies[3].start()
+        lax.fori_loop(0, 3, step_t, 0)
         return copies
 
     def fine_inner(start, vec):
@@ -233,7 +235,7 @@
 
         lax.fori_loop(0, 4, step, 0)
 
-    def fine_outer(vec, n, out):
+    def fine_outer(vec, n, out, keep):
         def step(t, carry):
             ahead = jnp.where(t == 3, top[0], 1.0)
             behind = jnp.where(t == 0, bottom[0], 1.0)
@@ -261,8 +263,14 @@
             )
             total = add_hop(total, back, 2, 1)
             for spin in range(4):
-                out[0, spin, :, t] = part[0, spin, :, t] + 0.5 * total[spin][0]
-                out[1, spin, :, t] = part[1, spin, :, t] + 0.5 * total[spin][1]
+                for q in range(2):
+                    value = part[q, spin, :, t] + 0.5 * total[spin][q]
+                    out[q, spin, :, t] = value
+                    if keep:
+                        start = pl.multiple_of(4 * t, 4)
+                        for z in range(2):
+                            for colour in range(3):
+                                wide[z, q, 3 * spin + colour, pl.ds(start, 4)] = value[colour, 4 * z : 4 * z + 4]
             return carry
 
         lax.fori_loop(0, 4, step, 0)
@@ -275,180 +283,153 @@
     fine_inner(source, iterate)
 
     loads[4].wait()
-    gap = jnp.zeros((2, 8, 8), F32)
+    gap = jnp.zeros((8, 8), F32)
 
     def pack_step(k, carry):
-        for p in range(2):
-            for group in range(6):
-                pieces = []
-                for c in range(4):
-                    pieces += [coarse_b[k, p, 4 * group + c], gap]
-                packed[k, p, group] = jnp.concatenate(pieces, axis=-1)
+        for i in range(NV):
+            pieces = []
+            for p in range(2):
+                for z in range(2):
+                    pieces += [coarse_b[k, p, i, z], gap]
+            packed[k, i] = jnp.concatenate(pieces, axis=-1)
         return carry
 
     lax.fori_loop(0, 9, pack_step, 0)
     loads[5].wait()
-
-    def widen_step(v, carry):
-        for k in range(2):
-            for p in range(2):
-                null_f[k, p, v] = null_b[k, p, v].astype(F32)
-        return carry
-
-    lax.fori_loop(0, NV, widen_step, 0)
-    rrep[...] = jnp.zeros_like(rrep)
+    rrow[...] = jnp.zeros_like(rrow)
     for copy in first:
         copy.wait_recv()
-    fine_outer(iterate, 0, res)
-
-    swapped = slot_ref[0] == 1
+    fine_outer(iterate, 0, res, True)
+
     row2 = lax.broadcasted_iota(jnp.int32, (8, 128), 0)
     lane2 = lax.broadcasted_iota(jnp.int32, (8, 128), 1)
     spread = (lane2 % 32 // 4 == row2).astype(F32)
 
-    def turn_step(s, carry):
-        spin, colour = s // 3, lax.rem(s, 3)
-        for q in range(2):
-            for pair in range(2):
-                first_t = res[q, spin, colour, 2 * pair].astype(jnp.bfloat16).astype(F32)
-                second_t = res[q, spin, colour, 2 * pair + 1].astype(jnp.bfloat16).astype(F32)
-                low = jnp.where(row2 < 4, first_t, pltpu.roll(second_t, 4, 0))
-                high = jnp.where(row2 < 4, pltpu.roll(first_t, 4, 0), second_t)
-                field[0, q, s, pair] = jnp.where(swapped, high, low)
-                field[1, q, s, pair] = jnp.where(swapped, low, high)
+    def round_step(s, carry):
+        for z in range(2):
+            re = wide[z, 0, s].astype(jnp.bfloat16)
+            im = wide[z, 1, s].astype(jnp.bfloat16)
+            field[z, 0, s] = re
+            field[z, 1, s] = im
+            field[z, 2, s] = -re
         return carry
 
-    lax.fori_loop(0, 12, turn_step, 0)
-
-    def restrict_step(i, carry):
-        k, v = i // NV, lax.rem(i, NV)
-        total_re = [None, None]
-        total_im = [None, None]
-        for s in range(12):
-            for pair in range(2):
-                nr = null_f[k, 0, v, s, 8 * pair : 8 * pair + 8]
-                ni = null_f[k, 1, v, s, 8 * pair : 8 * pair + 8]
-                fr = field[k, 0, s, pair]
-                fi = field[k, 1, s, pair]
-                re = nr * fr + ni * fi
-                im = nr * fi - ni * fr
-                total_re[pair] = re if s == 0 else total_re[pair] + re
-                total_im[pair] = im if s == 0 else total_im[pair] + im
-        racc[k, 0, v] = total_re[0] + total_re[1]
-        racc[k, 1, v] = total_im[0] + total_im[1]
-        return carry
-
-    lax.fori_loop(0, 2 * NV, restrict_step, 0)
-    tiles = []
-    for k in range(2):
-        for q in range(2):
-            summed = jnp.sum(racc[k, q], axis=1)
-            for c in range(4):
-                rrep[k, q, 32 * c : 32 * c + NV] = summed
-            tiles.append(
-                lax.dot_general(
-                    spread, rrep[k, q], (((1,), (1,)), ((), ())), precision=HIGHEST,
-                    preferred_element_type=F32,
-                )
-            )
-    rhs = [
-        [jnp.where(swapped, tiles[2 + p], tiles[p]) for p in range(2)],
-        [jnp.where(swapped, tiles[p], tiles[2 + p]) for p in range(2)],
-    ]
-
-    w = [[RELAX_WEIGHT * rhs[z][p] for p in range(2)] for z in range(2)]
-    lane6 = lax.broadcasted_iota(jnp.int32, (6, 8, 128), 2)
-    segment = lane2 // 32
+    lax.fori_loop(0, 12, round_step, 0)
+
+    def running(total, a, b):
+        product = a.astype(F32) * b.astype(F32)
+        return product if total is None else total + product
+
+    for z in range(2):
+        slot = slot_ref[z]
+
+        def restrict_step(i, carry):
+            totals = [[None, None], [None, None]]
+            for s in range(12):
+                for u in range(2):
+                    nr = null_b[slot, 0, 2 * i + u, s]
+                    ni = null_b[slot, 1, 2 * i + u, s]
+                    totals[u][0] = running(totals[u][0], nr, field[z, 0, s])
+                    totals[u][1] = running(totals[u][1], nr, field[z, 1, s])
+                    totals[u][0] = running(totals[u][0], ni, field[z, 1, s])
+                    totals[u][1] = running(totals[u][1], ni, field[z, 2, s])
+            for u in range(2):
+                for q in range(2):
+                    rrow[pl.ds(64 * q + 32 * z + 2 * i + u, 1)] = jnp.sum(totals[u][q], axis=0, keepdims=True)
+            return carry
+
+        lax.fori_loop(0, NV // 2, restrict_step, 0)
+
+    rhs = lax.dot_general(
+        spread, rrow[...], (((1,), (1,)), ((), ())), precision=HIGHEST, preferred_element_type=F32
+    )
+    w = RELAX_WEIGHT * rhs
+    lower_z = lane2 % 64 < 32
+    lower_p = lane2 < 64
+    parity = jnp.where(lower_p, 1.0, -1.0)
+
+    def accumulate(sums, k, vector):
+        blocks = packed[k]
+        re = blocks * (vector * parity)[None]
+        im = blocks * pltpu.roll(vector, 64, 1)[None]
+        return (re, im) if sums is None else (sums[0] + re, sums[1] + im)
+
+    def folded(low, high, distance):
+        lanes = lax.broadcasted_iota(jnp.int32, low.shape, low.ndim - 1)
+        clear = lanes // distance % 2 == 0
+        axis = low.ndim - 1
+        return jnp.where(clear, low, pltpu.roll(high, distance, axis)) + jnp.where(
+            clear, pltpu.roll(low, 128 - distance, axis), high
+        )
+
     sent = []
     for iteration in range(3):
-        for z in range(2):
-            for p in range(2):
-                wbuf[iteration, z, p] = w[z][p]
+        wbuf[iteration] = w
         phase = 1 + iteration
         copies = [
-            remote(phase, 0, wbuf.at[iteration], c_t.at[iteration, 0]),
-            remote(phase, 1, wbuf.at[iteration], c_t.at[iteration, 1]),
-            remote(phase, 2, wbuf.at[iteration, 0], c_z.at[iteration, 0]),
-            remote(phase, 3, wbuf.at[iteration, 1], c_z.at[iteration, 1]),
-            remote(phase, 4, wbuf.at[iteration], c_x.at[iteration, 0]),
-            remote(phase, 5, wbuf.at[iteration], c_x.at[iteration, 1]),
+            remote(phase, d, wbuf.at[iteration], c_halo.at[iteration, d]) for d in range(6)
         ]
         for copy in copies:
             copy.start()
         sent += copies
-        sums = [None, None]
-
-        def accumulate(z, k, vector):
-            lr = packed[k, 0, :, z]
-            li = packed[k, 1, :, z]
-            wr, wi = vector[0][None], vector[1][None]
-            re = lr * wr - li * wi
-            im = lr * wi + li * wr
-            sums[z] = (re, im) if sums[z] is None else (sums[z][0] + re, sums[z][1] + im)
-
-        for z in range(2):
-            accumulate(z, 0, w[z])
-            accumulate(z, 7, [pltpu.roll(a, 7, 0) for a in w[z]])
-            accumulate(z, 8, [pltpu.roll(a, 1, 0) for a in w[z]])
-        accumulate(0, 3, w[1])
-        accumulate(1, 4, w[0])
+        sums = accumulate(None, 0, w)
+        sums = accumulate(sums, 7, pltpu.roll(w, 7, 0))
+        sums = accumulate(sums, 8, pltpu.roll(w, 1, 0))
         for copy in copies:
             copy.wait_recv()
+        sums = accumulate(sums, 1, c_halo[iteration, 0])
+        sums = accumulate(sums, 2, c_halo[iteration, 1])
+        sums = accumulate(sums, 5, c_halo[iteration, 4])
+        sums = accumulate(sums, 6, c_halo[iteration, 5])
+        ahead = jnp.where(lower_z, pltpu.roll(w, 96, 1), pltpu.roll(c_halo[iteration, 2], 32, 1))
+        sums = accumulate(sums, 3, ahead)
+        behind = jnp.where(lower_z, pltpu.roll(c_halo[iteration, 3], 96, 1), pltpu.roll(w, 32, 1))
+        sums = accumulate(sums, 4, behind)
+        wide_p = lax.broadcasted_iota(jnp.int32, (NV, 8, 128), 2) < 64
+        folds = jnp.where(wide_p, sums[0], sums[1]) + pltpu.roll(jnp.where(wide_p, sums[1], sums[0]), 64, 2)
+        middle = folds[8:16]
+        bit = lax.broadcasted_iota(jnp.int32, (8, 8, 128), 2) // 16 % 2 == 0
+        middle = jnp.where(bit, middle + pltpu.roll(middle, 112, 2), 0.0)
+        folds = folded(folded(folds[0:8], folds[16:24], 16), middle, 8)
+        folds = folded(folds[0:4], folds[4:8], 4)
+        folds = folded(folds[0:2], folds[2:4], 2)
+        total = folded(folds[0], folds[1], 1)
+        w = w + RELAX_WEIGHT * (rhs - (2.0 * w + total))
+
+    coef[...] = jnp.dot(
+        jnp.transpose(w.astype(jnp.bfloat16).astype(F32)), spread, preferred_element_type=F32
+    )
+    def tile_step(v, carry):
         for z in range(2):
-            for k, ref in ((1, c_t.at[iteration, 0]), (2, c_t.at[iteration, 1]), (5, c_x.at[iteration, 0]), (6, c_x.at[iteration, 1])):
-                accumulate(z, k, (ref[z, 0], ref[z, 1]))
-        accumulate(1, 3, (c_z[iteration, 0, 0], c_z[iteration, 0, 1]))
-        accumulate(0, 4, (c_z[iteration, 1, 0], c_z[iteration, 1, 1]))
-        new = []
-        for z in range(2):
-            row_new = []
-            for p in range(2):
-                x = sums[z][p]
-                for shift in (16, 8, 4, 2, 1):
-                    x = x + pltpu.roll(x, 128 - shift, 2)
-                row_new.append(jnp.where(lane6 % 32 == 0, x, 0.0))
-            new.append(row_new)
-        w = [
-            [
-                w[z][p] + RELAX_WEIGHT * (rhs[z][p] - (2.0 * w[z][p] + gather_lanes(new[z][p], segment)))
-                for p in range(2)
-            ]
-            for z in range(2)
-        ]
+            re = jnp.broadcast_to(coef[pl.ds(32 * z + v, 1)], (16, 128))
+            im = jnp.broadcast_to(coef[pl.ds(64 + 32 * z + v, 1)], (16, 128))
+            for kind, value in enumerate((re, im, -im)):
+                tile[z, kind, v] = value.astype(jnp.bfloat16)
+        return carry
+
+    lax.fori_loop(0, NV, tile_step, 0)
 
     for z in range(2):
-        for p in range(2):
-            chosen = jnp.where(swapped, w[1 - z][p], w[z][p]).astype(jnp.bfloat16).astype(F32)
-            coef[z, p] = jnp.dot(
-                jnp.transpose(chosen), spread, precision=HIGHEST, preferred_element_type=F32
-            )
-
-    def prolong_step(s, carry):
-        spin, colour = s // 3, lax.rem(s, 3)
-        made = []
-        for k in range(2):
-            total_re = [None, None]
-            total_im = [None, None]
+        slot = slot_ref[z]
+
+        def prolong_step(i, carry):
+            totals = [[None, None], [None, None]]
             for v in range(NV):
-                cr = coef[k, 0, v : v + 1]
-                ci = coef[k, 1, v : v + 1]
-                for pair in range(2):
-                    nr = null_f[k, 0, v, s, 8 * pair : 8 * pair + 8]
-                    ni = null_f[k, 1, v, s, 8 * pair : 8 * pair + 8]
-                    re = nr * cr - ni * ci
-                    im = nr * ci + ni * cr
-                    total_re[pair] = re if v == 0 else total_re[pair] + re
-                    total_im[pair] = im if v == 0 else total_im[pair] + im
-            made.append((total_re, total_im))
-        for q in range(2):
-            for pair in range(2):
-                low = jnp.where(swapped, made[1][q][pair], made[0][q][pair])
-                high = jnp.where(swapped, made[0][q][pair], made[1][q][pair])
-                corr[q, spin, colour, 2 * pair] = jnp.where(row2 < 4, low, pltpu.roll(high, 4, 0))
-                corr[q, spin, colour, 2 * pair + 1] = jnp.where(row2 < 4, pltpu.roll(low, 4, 0), high)
-        return carry
-
-    lax.fori_loop(0, 12, prolong_step, 0)
+                for p in range(2):
+                    for u in range(2):
+                        null = null_b[slot, p, v, 2 * i + u]
+                        for q in range(2):
+                            kind = ((0, 2), (1, 0))[q][p]
+                            totals[u][q] = running(totals[u][q], null, tile[z, kind, v])
+            for u in range(2):
+                s = 2 * i + u
+                spin, colour = s // 3, lax.rem(s, 3)
+                for q in range(2):
+                    for t in range(4):
+                        corr[q, spin, colour, t, 4 * z : 4 * z + 4] = totals[u][q][4 * t : 4 * t + 4]
+            return carry
+
+        lax.fori_loop(0, 6, prolong_step, 0)
 
     second = fine_send(corr, 1)
 
@@ -457,36 +438,19 @@
         return carry
 
     lax.fori_loop(0, 4, add_step, 0)
-    store_x = pltpu.make_async_copy(out_x, out_x_h, local_sem.at[6])
-    store_x.start()
     fine_inner(res, corr)
     for copy in second:
         copy.wait_recv()
-    fine_outer(corr, 1, out_r)
-    store_r = pltpu.make_async_copy(out_r, out_r_h, local_sem.at[7])
-    store_r.start()
+    fine_outer(corr, 1, out_r, False)
     for copy in first + sent + second:
         copy.wait_send()
-    store_x.wait()
-    store_r.wait()
-
-
-def gather_lanes(x, segment):
-    y = x[0]
-    for group in range(1, 6):
-        y = y + pltpu.roll(x[group], 4 * group, 1)
-    placed = y
-    for c in range(1, 4):
-        placed = jnp.where(segment == c, pltpu.roll(y, c, 1), placed)
-    placed = placed + pltpu.roll(placed, 64, 1)
-    return placed + pltpu.roll(placed, 32, 1)
 
 
 def per_device(source, iterate, gauge_links, clover, bc_sign, null_store, block_slot, coarse_links):
     null = null_store.reshape((2, 2, NV, 12, 16, 128))
     coarse = jnp.transpose(coarse_links, (0, 1, 2, 4, 5, 6, 7, 3)).reshape((9, 2, NV, 2, 8, NV))
     slots = block_slot.reshape((2,))
-    spinor = jax.ShapeDtypeStruct((2, 4, 3, 4, 8, 128), F32)
+    spinor = pltpu.VMEM((2, 4, 3, 4, 8, 128), F32)
     anywhere = pl.BlockSpec(memory_space=pl.ANY)
     scalars = pl.BlockSpec(memory_space=pltpu.SMEM)
     half = (2, 2, 3, 8, 128)
@@ -495,23 +459,22 @@
         kernel,
         out_shape=(spinor, spinor),
         in_specs=[anywhere] * 6 + [scalars] * 2,
-        out_specs=(anywhere, anywhere),
+        out_specs=(pl.BlockSpec(memory_space=pltpu.VMEM),) * 2,
         scratch_shapes=[
             vmem(*spinor.shape), vmem(*spinor.shape), vmem(4, 2, 3, 3, 4, 8, 128),
             vmem(2, 2, 6, 6, 4, 8, 128), pltpu.VMEM((2, 2, NV, 12, 16, 128), jnp.bfloat16),
-            vmem(9, 2, NV, 2, 8, NV), vmem(2, 2, NV, 12, 16, 128), vmem(9, 2, 6, 2, 8, 128),
+            vmem(9, 2, NV, 2, 8, NV), vmem(9, NV, 8, 128),
             vmem(2, 5, *half), vmem(2, 5, *half), vmem(4, *half), vmem(4, *half),
             vmem(2, 4, 2, 2, 3, 1, 128), vmem(2, 4, 2, 2, 3, 1, 128), vmem(2, *half), vmem(2, *half),
             vmem(2, 4, 2, 2, 3, 1, 128), vmem(2, 4, 2, 2, 3, 1, 128), vmem(2, *half), vmem(2, *half),
-            vmem(*spinor.shape), vmem(*spinor.shape), vmem(*spinor.shape), vmem(*spinor.shape),
-            vmem(*spinor.shape), vmem(2, 2, 12, 2, 8, 128), vmem(2, 2, NV, 8, 128),
-            vmem(2, 2, 128, 128), vmem(2, 2, 128, 128), vmem(3, 2, 2, 8, 128),
-            vmem(3, 2, 2, 2, 8, 128), vmem(3, 2, 2, 8, 128), vmem(3, 2, 2, 2, 8, 128),
-            pltpu.SemaphoreType.DMA((8,)), pltpu.SemaphoreType.DMA((5, 6)),
+            vmem(*spinor.shape), vmem(*spinor.shape), vmem(*spinor.shape), vmem(2, 2, 12, 16, 128),
+            pltpu.VMEM((2, 3, 12, 16, 128), jnp.bfloat16), vmem(128, 128), vmem(128, 128),
+            pltpu.VMEM((2, 3, NV, 16, 128), jnp.bfloat16), vmem(3, 8, 128), vmem(3, 6, 8, 128),
+            pltpu.SemaphoreType.DMA((6,)), pltpu.SemaphoreType.DMA((5, 6)),
             pltpu.SemaphoreType.DMA((5, 6)),
         ],
         compiler_params=pltpu.CompilerParams(
-            collective_id=0, has_side_effects=True, vmem_limit_bytes=60 * 1024 * 1024
+            collective_id=0, has_side_effects=True, vmem_limit_bytes=56 * 1024 * 1024
         ),
     )(source, iterate, gauge_links, clover, null, coarse, bc_sign, slots)
 

time: 39.4 us -> 32.5 us (0.82)
  Pallas kernels: 35.1 us -> 30.2 us
  local copies, waits for them, and re-layouts: 3.53 us -> 1.49 us
    pallas_call x1, Pallas kernels: 35.1 us -> 30.2 us  [per_device(): pl.pallas_call(kernel, out_shape=(spinor, spinor), in_specs=[anywhere] *...]
    unnamed x2, local copies, waits for them, and re-layouts: 3.53 us -> 1.49 us
where the time goes in v1:
time: 32.5 us; the launch traced here: 32.4 us
  Pallas kernels  30.2 us (93%)
  local copies, waits for them, and re-layouts  1.49 us (5%)
  between operations  0.64 us (2%)
    pallas_call x1, Pallas kernels, per_device(): pl.pallas_call(kernel, out_shape=(spinor, spinor), in_specs=[anywhere] *...  30.2 us
    unnamed x2, local copies, waits for them, and re-layouts  1.49 us

profile of v1, /device:TPU:1, one launch (start us, length us, event | category | flops | bytes accessed | tf_op | source)
XLA Modules:
  0.0 32.4 jit_solution(13686216301301590251)
XLA Ops:
  0.6 30.2 %shard_map.95 = (f32[2,4,3,4,8,128]{5,4,3,2,1,0:T(8,128)S(1)}, f32[2,4,3,4,8,128]{5,4,3,2,1,0:T(8,128)S(1)}) custom-call(f32[2,4,3,4,8,128]{5,4,3,2,1,0:T(8,128)} %source_h.1, f32[2,4,3,4,8,128]{5,4,3,2,1,0:T(8,128)} %iterate_h.1, f32[4,2,3,3,4,8,128]{6,5,4,3,2,1,0:T(8,128)} %links_h.1, f32[2,2,6,6,4,8,128]{6,5,4,3,2,1,0:T(8,128)} %clover_h.1, ...), custom_call_target="tpu_custom_call" | custom-call | tf_op jit(solution)/shard_map/pallas_call | solution.py:458
  30.9 0.7 %copy.13 = f32[2,4,3,4,8,128]{5,4,3,2,1,0:T(8,128)} copy(f32[2,4,3,4,8,128]{5,4,3,2,1,0:T(8,128)S(1)} %get-tuple-element.2) | data formatting | bytes 786432
  31.6 0.7 %copy.14 = f32[2,4,3,4,8,128]{5,4,3,2,1,0:T(8,128)} copy(f32[2,4,3,4,8,128]{5,4,3,2,1,0:T(8,128)S(1)} %get-tuple-element.3) | data formatting | bytes 786432

commit v2 on v1

--- a/solution.py
+++ b/solution.py
@@ -94,12 +94,12 @@
 
 
 def kernel(
-    source_h, iterate_h, links_h, clover_h, null_h, coarse_h, bc_ref, slot_ref,
+    source_h, iterate_h, links_h, clover_h, null_h, coarse_h, bc_h, slot_h,
     out_x, out_r,
     source, iterate, links, clover, null_b, coarse_b, packed,
     ht, gt, gz, gx, hz_s, gz_s, hx_s, gx_s, hz_r, gz_r, hx_r, gx_r,
     part, res, corr, wide, field, rrow, coef, tile, wbuf,
-    c_halo, local_sem, send_sem, recv_sem,
+    c_halo, bc_ref, slot_ref, local_sem, send_sem, recv_sem,
 ):
     me = (lax.axis_index("ta"), lax.axis_index("gz"), lax.axis_index("xy"))
     size = (lax.axis_size("ta"), lax.axis_size("gz"), lax.axis_size("xy"))
@@ -112,12 +112,13 @@
     loads = [
         pltpu.make_async_copy(source_from, into, local_sem.at[i])
         for i, (source_from, into) in enumerate((
-            (iterate_h, iterate), (links_h, links), (clover_h, clover), (source_h, source),
-            (coarse_h, coarse_b), (null_h, null_b),
+            (iterate_h, iterate), (links_h.at[0:3], links.at[0:3]), (clover_h, clover), (source_h, source),
+            (coarse_h, coarse_b), (null_h, null_b), (links_h.at[3], links.at[3]),
+            (bc_h, bc_ref), (slot_h, slot_ref),
         ))
     ]
-    for load in loads:
-        load.start()
+    loads[0].start()
+    loads[1].start()
     barrier = pltpu.get_barrier_semaphore()
     for axis in range(3):
         for step in (-1, 1):
@@ -129,10 +130,6 @@
 
     def sign_of(mu, at_edge):
         return jnp.where(at_edge, bc_ref[mu], 1).astype(F32)
-
-    top = [sign_of(axis, me[axis] == size[axis] - 1) for axis in range(3)]
-    bottom = [sign_of(axis, me[axis] == 0) for axis in range(3)]
-    sign_y = bc_ref[3].astype(F32)
 
     def remote(phase, d, source_from, into):
         return pltpu.make_async_remote_copy(
@@ -163,18 +160,20 @@
     def fine_send(vec, n):
         copies = fine_copies(n)
 
-        def step_x(t, carry):
-            shift_up = t * 32
-            half = project(vec, t, 2, -1)
-            here = lane // 32 == t
-            old = load_half(hx_s, (n,))
-            store_half(hx_s, (n,), both(half, old, lambda a, b: jnp.where(here, pltpu.roll(a, shift_up, 2), b)))
-            back = times_dagger(links, 2, t, project(vec, t, 2, 1))
-            store_half(gx, (t,), back)
-            shift_down = lax.rem(t * 32 + 32, 128)
-            old = load_half(gx_s, (n,))
-            store_half(gx_s, (n,), both(back, old, lambda a, b: jnp.where(here, pltpu.roll(a, shift_down, 2), b)))
-            return carry
+        def send_x():
+            ahead = None
+            behind = None
+            for t in range(4):
+                here = lane // 32 == t
+                half = project(vec, t, 2, -1)
+                back = times_dagger(links, 2, t, project(vec, t, 2, 1))
+                store_half(gx, (t,), back)
+                half = each(half, lambda a: pltpu.roll(a, 32 * t, 2) if t else a)
+                back = each(back, lambda a: pltpu.roll(a, (32 * t + 32) % 128, 2) if t < 3 else a)
+                ahead = half if t == 0 else both(half, ahead, lambda a, b: jnp.where(here, a, b))
+                behind = back if t == 0 else both(back, behind, lambda a, b: jnp.where(here, a, b))
+            store_half(hx_s, (n,), ahead)
+            store_half(gx_s, (n,), behind)
 
         def step_t(t, carry):
             store_half(ht, (n, t + 1), project(vec, t + 1, 0, -1))
@@ -195,10 +194,11 @@
             pl.semaphore_wait(barrier, 6)
         copies[0].start()
         copies[1].start()
-        lax.fori_loop(0, 4, step_x, 0)
+        send_x()
         copies[4].start()
         copies[5].start()
-        lax.fori_loop(0, 4, step_z, 0)
+        for t in range(4):
+            step_z(t, 0)
         copies[2].start()
         copies[3].start()
         lax.fori_loop(0, 3, step_t, 0)
@@ -277,9 +277,15 @@
 
     loads[0].wait()
     loads[1].wait()
+    for i in (7, 8, 6, 2, 3, 4, 5):
+        loads[i].start()
     first = fine_send(iterate, 0)
-    loads[2].wait()
+    for i in (7, 8, 6, 2):
+        loads[i].wait()
     loads[3].wait()
+    top = [sign_of(axis, me[axis] == size[axis] - 1) for axis in range(3)]
+    bottom = [sign_of(axis, me[axis] == 0) for axis in range(3)]
+    sign_y = bc_ref[3].astype(F32)
     fine_inner(source, iterate)
 
     loads[4].wait()
@@ -324,21 +330,23 @@
         slot = slot_ref[z]
 
         def restrict_step(i, carry):
-            totals = [[None, None], [None, None]]
-            for s in range(12):
+            for j in range(2):
+                first_v = 4 * i + 2 * j
+                totals = [[None, None], [None, None]]
+                for s in range(12):
+                    for u in range(2):
+                        nr = null_b[slot, 0, first_v + u, s]
+                        ni = null_b[slot, 1, first_v + u, s]
+                        totals[u][0] = running(totals[u][0], nr, field[z, 0, s])
+                        totals[u][1] = running(totals[u][1], nr, field[z, 1, s])
+                        totals[u][0] = running(totals[u][0], ni, field[z, 1, s])
+                        totals[u][1] = running(totals[u][1], ni, field[z, 2, s])
                 for u in range(2):
-                    nr = null_b[slot, 0, 2 * i + u, s]
-                    ni = null_b[slot, 1, 2 * i + u, s]
-                    totals[u][0] = running(totals[u][0], nr, field[z, 0, s])
-                    totals[u][1] = running(totals[u][1], nr, field[z, 1, s])
-                    totals[u][0] = running(totals[u][0], ni, field[z, 1, s])
-                    totals[u][1] = running(totals[u][1], ni, field[z, 2, s])
-            for u in range(2):
-                for q in range(2):
-                    rrow[pl.ds(64 * q + 32 * z + 2 * i + u, 1)] = jnp.sum(totals[u][q], axis=0, keepdims=True)
-            return carry
-
-        lax.fori_loop(0, NV // 2, restrict_step, 0)
+                    for q in range(2):
+                        rrow[pl.ds(64 * q + 32 * z + first_v + u, 1)] = jnp.sum(totals[u][q], axis=0, keepdims=True)
+            return carry
+
+        lax.fori_loop(0, NV // 4, restrict_step, 0)
 
     rhs = lax.dot_general(
         spread, rrow[...], (((1,), (1,)), ((), ())), precision=HIGHEST, preferred_element_type=F32
@@ -375,16 +383,15 @@
         sums = accumulate(None, 0, w)
         sums = accumulate(sums, 7, pltpu.roll(w, 7, 0))
         sums = accumulate(sums, 8, pltpu.roll(w, 1, 0))
-        for copy in copies:
-            copy.wait_recv()
-        sums = accumulate(sums, 1, c_halo[iteration, 0])
-        sums = accumulate(sums, 2, c_halo[iteration, 1])
-        sums = accumulate(sums, 5, c_halo[iteration, 4])
-        sums = accumulate(sums, 6, c_halo[iteration, 5])
+        copies[2].wait_recv()
+        copies[3].wait_recv()
         ahead = jnp.where(lower_z, pltpu.roll(w, 96, 1), pltpu.roll(c_halo[iteration, 2], 32, 1))
         sums = accumulate(sums, 3, ahead)
         behind = jnp.where(lower_z, pltpu.roll(c_halo[iteration, 3], 96, 1), pltpu.roll(w, 32, 1))
         sums = accumulate(sums, 4, behind)
+        for k, d in ((1, 0), (2, 1), (5, 4), (6, 5)):
+            copies[d].wait_recv()
+            sums = accumulate(sums, k, c_halo[iteration, d])
         wide_p = lax.broadcasted_iota(jnp.int32, (NV, 8, 128), 2) < 64
         folds = jnp.where(wide_p, sums[0], sums[1]) + pltpu.roll(jnp.where(wide_p, sums[1], sums[0]), 64, 2)
         middle = folds[8:16]
@@ -452,13 +459,12 @@
     slots = block_slot.reshape((2,))
     spinor = pltpu.VMEM((2, 4, 3, 4, 8, 128), F32)
     anywhere = pl.BlockSpec(memory_space=pl.ANY)
-    scalars = pl.BlockSpec(memory_space=pltpu.SMEM)
     half = (2, 2, 3, 8, 128)
     vmem = lambda *shape: pltpu.VMEM(shape, F32)
     return pl.pallas_call(
         kernel,
         out_shape=(spinor, spinor),
-        in_specs=[anywhere] * 6 + [scalars] * 2,
+        in_specs=[anywhere] * 8,
         out_specs=(pl.BlockSpec(memory_space=pltpu.VMEM),) * 2,
         scratch_shapes=[
             vmem(*spinor.shape), vmem(*spinor.shape), vmem(4, 2, 3, 3, 4, 8, 128),
@@ -470,7 +476,7 @@
             vmem(*spinor.shape), vmem(*spinor.shape), vmem(*spinor.shape), vmem(2, 2, 12, 16, 128),
             pltpu.VMEM((2, 3, 12, 16, 128), jnp.bfloat16), vmem(128, 128), vmem(128, 128),
             pltpu.VMEM((2, 3, NV, 16, 128), jnp.bfloat16), vmem(3, 8, 128), vmem(3, 6, 8, 128),
-            pltpu.SemaphoreType.DMA((6,)), pltpu.SemaphoreType.DMA((5, 6)),
+            pltpu.SMEM((4,), jnp.int32), pltpu.SMEM((2,), jnp.int32), pltpu.SemaphoreType.DMA((9,)), pltpu.SemaphoreType.DMA((5, 6)),
             pltpu.SemaphoreType.DMA((5, 6)),
         ],
         compiler_params=pltpu.CompilerParams(

time: 32.5 us -> 31.5 us (0.969)
  Pallas kernels: 30.2 us -> 29.2 us
    pallas_call x1, Pallas kernels: 30.2 us -> 29.2 us  [per_device(): pl.pallas_call(kernel, out_shape=(spinor, spinor), in_specs=[anywhere] *...]
where the time goes in v2:
time: 31.5 us; the launch traced here: 31.3 us
  Pallas kernels  29.2 us (93%)
  local copies, waits for them, and re-layouts  1.49 us (5%)
  between operations  0.64 us (2%)
    pallas_call x1, Pallas kernels, per_device(): pl.pallas_call(kernel, out_shape=(spinor, spinor), in_specs=[anywhere] *...  29.2 us
    unnamed x2, local copies, waits for them, and re-layouts  1.49 us

profile of v2, /device:TPU:1, one launch (start us, length us, event | category | flops | bytes accessed | tf_op | source)
XLA Modules:
  0.0 31.3 jit_solution(12413707743168057684)
XLA Ops:
  0.6 29.2 %shard_map.95 = (f32[2,4,3,4,8,128]{5,4,3,2,1,0:T(8,128)S(1)}, f32[2,4,3,4,8,128]{5,4,3,2,1,0:T(8,128)S(1)}) custom-call(f32[2,4,3,4,8,128]{5,4,3,2,1,0:T(8,128)} %source_h.1, f32[2,4,3,4,8,128]{5,4,3,2,1,0:T(8,128)} %iterate_h.1, f32[4,2,3,3,4,8,128]{6,5,4,3,2,1,0:T(8,128)} %links_h.1, f32[2,2,6,6,4,8,128]{6,5,4,3,2,1,0:T(8,128)} %clover_h.1, ...), custom_call_target="tpu_custom_call" | custom-call | tf_op jit(solution)/shard_map/pallas_call | solution.py:464
  29.8 0.7 %copy.13 = f32[2,4,3,4,8,128]{5,4,3,2,1,0:T(8,128)} copy(f32[2,4,3,4,8,128]{5,4,3,2,1,0:T(8,128)S(1)} %get-tuple-element.2) | data formatting | bytes 786432
  30.6 0.7 %copy.14 = f32[2,4,3,4,8,128]{5,4,3,2,1,0:T(8,128)} copy(f32[2,4,3,4,8,128]{5,4,3,2,1,0:T(8,128)S(1)} %get-tuple-element.3) | data formatting | bytes 786432

commit v3 on v2

--- a/solution.py
+++ b/solution.py
@@ -44,6 +44,20 @@
     for b in range(3):
         ur = links[mu, 0, :, b, t]
         ui = links[mu, 1, :, b, t]
+        for s in range(2):
+            br = half[s][0][b][None]
+            bi = half[s][1][b][None]
+            re = ur * br - ui * bi
+            im = ur * bi + ui * br
+            out[s] = (re, im) if b == 0 else (out[s][0] + re, out[s][1] + im)
+    return out
+
+
+def times_packed(block, half):
+    out = [None, None]
+    for b in range(3):
+        ur = block[0, :, b]
+        ui = block[1, :, b]
         for s in range(2):
             br = half[s][0][b][None]
             bi = half[s][1][b][None]
@@ -97,7 +111,7 @@
     source_h, iterate_h, links_h, clover_h, null_h, coarse_h, bc_h, slot_h,
     out_x, out_r,
     source, iterate, links, clover, null_b, coarse_b, packed,
-    ht, gt, gz, gx, hz_s, gz_s, hx_s, gx_s, hz_r, gz_r, hx_r, gx_r,
+    ht_s, gt_s, ht_r, gt_r, ux, uz, rz, gz, gx, hz_s, gz_s, hx_s, gx_s, hz_r, gz_r, hx_r, gx_r,
     part, res, corr, wide, field, rrow, coef, tile, wbuf,
     c_halo, bc_ref, slot_ref, local_sem, send_sem, recv_sem,
 ):
@@ -149,8 +163,8 @@
     def fine_copies(n):
         phase = 4 * n
         return [
-            remote(phase, 0, ht.at[n, 0], ht.at[n, 4]),
-            remote(phase, 1, gt.at[n, 4], gt.at[n, 0]),
+            remote(phase, 0, ht_s.at[n], ht_r.at[n]),
+            remote(phase, 1, gt_s.at[n], gt_r.at[n]),
             remote(phase, 2, hz_s.at[n], hz_r.at[n]),
             remote(phase, 3, gz_s.at[n], gz_r.at[n]),
             remote(phase, 4, hx_s.at[n], hx_r.at[n]),
@@ -175,21 +189,18 @@
             store_half(hx_s, (n,), ahead)
             store_half(gx_s, (n,), behind)
 
-        def step_t(t, carry):
-            store_half(ht, (n, t + 1), project(vec, t + 1, 0, -1))
-            store_half(gt, (n, t + 1), times_dagger(links, 0, t, project(vec, t, 0, 1)))
-            return carry
-
         def step_z(t, carry):
             half = project(vec, t, 1, -1)
-            store_half(hz_s, (n, t), each(half, lambda a: a[:, 0:1, :]))
+            for s in range(2):
+                for q in range(2):
+                    hz_s[n, q, s, :, t : t + 1, :] = half[s][q][:, 0:1, :]
             back = times_dagger(links, 1, t, project(vec, t, 1, 1))
             store_half(gz, (t,), back)
             store_half(gz_s, (n, t), each(back, lambda a: a[:, 7:8, :]))
             return carry
 
-        store_half(ht, (n, 0), project(vec, 0, 0, -1))
-        store_half(gt, (n, 4), times_dagger(links, 0, 3, project(vec, 3, 0, 1)))
+        store_half(ht_s, (n,), project(vec, 0, 0, -1))
+        store_half(gt_s, (n,), times_dagger(links, 0, 3, project(vec, 3, 0, 1)))
         if n == 0:
             pl.semaphore_wait(barrier, 6)
         copies[0].start()
@@ -201,7 +212,6 @@
             step_z(t, 0)
         copies[2].start()
         copies[3].start()
-        lax.fori_loop(0, 3, step_t, 0)
         return copies
 
     def fine_inner(start, vec):
@@ -233,51 +243,78 @@
                     part[1, spin, :, t] = start[1, spin, :, t] - MASS_TERM * vi - out_im[s] + 0.5 * total[spin][1]
             return carry
 
-        lax.fori_loop(0, 4, step, 0)
-
-    def fine_outer(vec, n, out, keep):
-        def step(t, carry):
-            ahead = jnp.where(t == 3, top[0], 1.0)
-            behind = jnp.where(t == 0, bottom[0], 1.0)
-            half = each(load_half(ht, (n, t + 1)), lambda a: a * ahead)
-            total = add_hop(None, times_link(links, 0, t, half), 0, -1)
-            total = add_hop(total, each(load_half(gt, (n, t)), lambda a: a * behind), 0, 1)
-            edge = load_half(hz_r, (n, t))
-            half = both(project(vec, t, 1, -1), edge, lambda a, b: jnp.where(row == 7, b * top[1], pltpu.roll(a, 7, 1)))
-            total = add_hop(total, times_link(links, 1, t, half), 1, -1)
-            edge = load_half(gz_r, (n, t))
-            back = both(load_half(gz, (t,)), edge, lambda a, b: jnp.where(row == 0, b * bottom[1], pltpu.roll(a, 1, 1)))
-            total = add_hop(total, back, 1, 1)
-            shift = 96 - 32 * t
-            edge = load_half(hx_r, (n,))
-            half = both(
-                project(vec, t, 2, -1), edge,
-                lambda a, b: jnp.where(lane >= 96, pltpu.roll(b, shift, 2) * top[2], pltpu.roll(a, 96, 2)),
-            )
-            total = add_hop(total, times_link(links, 2, t, half), 2, -1)
-            shift_back = lax.rem(128 - 32 * t, 128)
-            edge = load_half(gx_r, (n,))
-            back = both(
-                load_half(gx, (t,)), edge,
-                lambda a, b: jnp.where(lane < 32, pltpu.roll(b, shift_back, 2) * bottom[2], pltpu.roll(a, 32, 2)),
-            )
-            total = add_hop(total, back, 2, 1)
+        def add_part(t, total):
             for spin in range(4):
                 for q in range(2):
-                    value = part[q, spin, :, t] + 0.5 * total[spin][q]
+                    part[q, spin, :, t] = part[q, spin, :, t] + 0.5 * total[spin][q]
+
+        def step_zx(t, carry):
+            half = each(project(vec, t, 1, -1), lambda a: jnp.where(row == 7, 0.0, pltpu.roll(a, 7, 1)))
+            total = add_hop(None, times_link(links, 1, t, half), 1, -1)
+            back = each(load_half(gz, (t,)), lambda a: jnp.where(row == 0, 0.0, pltpu.roll(a, 1, 1)))
+            total = add_hop(total, back, 1, 1)
+            half = each(project(vec, t, 2, -1), lambda a: jnp.where(lane >= 96, 0.0, pltpu.roll(a, 96, 2)))
+            total = add_hop(total, times_link(links, 2, t, half), 2, -1)
+            back = each(load_half(gx, (t,)), lambda a: jnp.where(lane < 32, 0.0, pltpu.roll(a, 32, 2)))
+            add_part(t, add_hop(total, back, 2, 1))
+            return carry
+
+        def step_t(t, carry):
+            add_part(t, add_hop(None, times_link(links, 0, t, project(vec, t + 1, 0, -1)), 0, -1))
+            add_part(t + 1, add_hop(None, times_dagger(links, 0, t, project(vec, t, 0, 1)), 0, 1))
+            return carry
+
+        lax.fori_loop(0, 4, step, 0)
+        lax.fori_loop(0, 4, step_zx, 0)
+        lax.fori_loop(0, 3, step_t, 0)
+
+    def prepare_edges():
+        lane9 = lax.broadcasted_iota(jnp.int32, (3, 3, 8, 128), 3)
+        for p in range(2):
+            gathered = None
+            for t in range(4):
+                block = links[2, p, :, :, t]
+                if t < 3:
+                    block = pltpu.roll(block, (32 * t + 32) % 128, 3)
+                gathered = block if t == 0 else jnp.where(lane9 // 32 == t, block, gathered)
+                uz[p, :, :, t : t + 1, :] = links[1, p, :, :, t, 7:8, :]
+            ux[p] = gathered
+
+    def fine_outer(vec, n, out, keep):
+        def scaled(half, sign):
+            factor = 0.5 * sign
+            return each(half, lambda a: a * factor)
+
+        ahead_t = times_link(links, 0, 3, scaled(load_half(ht_r, (n,)), top[0]))
+        behind_t = scaled(load_half(gt_r, (n,)), bottom[0])
+        ahead_x = times_packed(ux, scaled(load_half(hx_r, (n,)), top[2]))
+        behind_x = scaled(load_half(gx_r, (n,)), bottom[2])
+        store_half(rz, (), times_packed(uz, scaled(load_half(hz_r, (n,)), top[1])))
+        for t in range(4):
+            half = each(ahead_x, lambda a: jnp.where(lane >= 96, pltpu.roll(a, 96 - 32 * t, 2) if t < 3 else a, 0.0))
+            total = add_hop(None, half, 2, -1)
+            half = each(behind_x, lambda a: jnp.where(lane < 32, pltpu.roll(a, 128 - 32 * t, 2) if t else a, 0.0))
+            total = add_hop(total, half, 2, 1)
+            half = [(rz[0, s, :, t : t + 1, :], rz[1, s, :, t : t + 1, :]) for s in range(2)]
+            total = add_hop(total, each(half, lambda a: jnp.where(row == 7, a, 0.0)), 1, -1)
+            half = scaled(load_half(gz_r, (n, t)), bottom[1])
+            total = add_hop(total, each(half, lambda a: jnp.where(row == 0, a, 0.0)), 1, 1)
+            if t == 3:
+                total = add_hop(total, ahead_t, 0, -1)
+            if t == 0:
+                total = add_hop(total, behind_t, 0, 1)
+            for spin in range(4):
+                for q in range(2):
+                    value = part[q, spin, :, t] + total[spin][q]
                     out[q, spin, :, t] = value
                     if keep:
-                        start = pl.multiple_of(4 * t, 4)
                         for z in range(2):
                             for colour in range(3):
-                                wide[z, q, 3 * spin + colour, pl.ds(start, 4)] = value[colour, 4 * z : 4 * z + 4]
-            return carry
-
-        lax.fori_loop(0, 4, step, 0)
+                                wide[z, q, 3 * spin + colour, 4 * t : 4 * t + 4] = value[colour, 4 * z : 4 * z + 4]
 
     loads[0].wait()
     loads[1].wait()
-    for i in (7, 8, 6, 2, 3, 4, 5):
+    for i in (7, 8, 6, 2, 3, 5, 4):
         loads[i].start()
     first = fine_send(iterate, 0)
     for i in (7, 8, 6, 2):
@@ -286,21 +323,9 @@
     top = [sign_of(axis, me[axis] == size[axis] - 1) for axis in range(3)]
     bottom = [sign_of(axis, me[axis] == 0) for axis in range(3)]
     sign_y = bc_ref[3].astype(F32)
+    prepare_edges()
     fine_inner(source, iterate)
 
-    loads[4].wait()
-    gap = jnp.zeros((8, 8), F32)
-
-    def pack_step(k, carry):
-        for i in range(NV):
-            pieces = []
-            for p in range(2):
-                for z in range(2):
-                    pieces += [coarse_b[k, p, i, z], gap]
-            packed[k, i] = jnp.concatenate(pieces, axis=-1)
-        return carry
-
-    lax.fori_loop(0, 9, pack_step, 0)
     loads[5].wait()
     rrow[...] = jnp.zeros_like(rrow)
     for copy in first:
@@ -320,7 +345,8 @@
             field[z, 2, s] = -re
         return carry
 
-    lax.fori_loop(0, 12, round_step, 0)
+    for s in range(12):
+        round_step(s, 0)
 
     def running(total, a, b):
         product = a.astype(F32) * b.astype(F32)
@@ -330,8 +356,8 @@
         slot = slot_ref[z]
 
         def restrict_step(i, carry):
-            for j in range(2):
-                first_v = 4 * i + 2 * j
+            for j in range(4):
+                first_v = 8 * i + 2 * j
                 totals = [[None, None], [None, None]]
                 for s in range(12):
                     for u in range(2):
@@ -346,7 +372,7 @@
                         rrow[pl.ds(64 * q + 32 * z + first_v + u, 1)] = jnp.sum(totals[u][q], axis=0, keepdims=True)
             return carry
 
-        lax.fori_loop(0, NV // 4, restrict_step, 0)
+        lax.fori_loop(0, NV // 8, restrict_step, 0)
 
     rhs = lax.dot_general(
         spread, rrow[...], (((1,), (1,)), ((), ())), precision=HIGHEST, preferred_element_type=F32
@@ -369,6 +395,17 @@
         return jnp.where(clear, low, pltpu.roll(high, distance, axis)) + jnp.where(
             clear, pltpu.roll(low, 128 - distance, axis), high
         )
+
+    gap = jnp.zeros((8, 8), F32)
+
+    def pack_step(k, carry):
+        for i in range(NV):
+            pieces = []
+            for p in range(2):
+                for z in range(2):
+                    pieces += [coarse_b[k, p, i, z], gap]
+            packed[k, i] = jnp.concatenate(pieces, axis=-1)
+        return carry
 
     sent = []
     for iteration in range(3):
@@ -380,6 +417,9 @@
         for copy in copies:
             copy.start()
         sent += copies
+        if iteration == 0:
+            loads[4].wait()
+            lax.fori_loop(0, 9, pack_step, 0)
         sums = accumulate(None, 0, w)
         sums = accumulate(sums, 7, pltpu.roll(w, 7, 0))
         sums = accumulate(sums, 8, pltpu.roll(w, 1, 0))
@@ -414,7 +454,8 @@
                 tile[z, kind, v] = value.astype(jnp.bfloat16)
         return carry
 
-    lax.fori_loop(0, NV, tile_step, 0)
+    for v in range(NV):
+        tile_step(v, 0)
 
     for z in range(2):
         slot = slot_ref[z]
@@ -436,7 +477,11 @@
                         corr[q, spin, colour, t, 4 * z : 4 * z + 4] = totals[u][q][4 * t : 4 * t + 4]
             return carry
 
-        lax.fori_loop(0, 6, prolong_step, 0)
+        def prolong_pair(i, carry):
+            prolong_step(2 * i, carry)
+            return prolong_step(2 * i + 1, carry)
+
+        lax.fori_loop(0, 3, prolong_pair, 0)
 
     second = fine_send(corr, 1)
 
@@ -470,9 +515,10 @@
             vmem(*spinor.shape), vmem(*spinor.shape), vmem(4, 2, 3, 3, 4, 8, 128),
             vmem(2, 2, 6, 6, 4, 8, 128), pltpu.VMEM((2, 2, NV, 12, 16, 128), jnp.bfloat16),
             vmem(9, 2, NV, 2, 8, NV), vmem(9, NV, 8, 128),
-            vmem(2, 5, *half), vmem(2, 5, *half), vmem(4, *half), vmem(4, *half),
-            vmem(2, 4, 2, 2, 3, 1, 128), vmem(2, 4, 2, 2, 3, 1, 128), vmem(2, *half), vmem(2, *half),
-            vmem(2, 4, 2, 2, 3, 1, 128), vmem(2, 4, 2, 2, 3, 1, 128), vmem(2, *half), vmem(2, *half),
+            vmem(2, *half), vmem(2, *half), vmem(2, *half), vmem(2, *half),
+            vmem(2, 3, 3, 8, 128), vmem(2, 3, 3, 4, 128), vmem(2, 2, 3, 4, 128), vmem(4, *half), vmem(4, *half),
+            vmem(2, 2, 2, 3, 4, 128), vmem(2, 4, 2, 2, 3, 1, 128), vmem(2, *half), vmem(2, *half),
+            vmem(2, 2, 2, 3, 4, 128), vmem(2, 4, 2, 2, 3, 1, 128), vmem(2, *half), vmem(2, *half),
             vmem(*spinor.shape), vmem(*spinor.shape), vmem(*spinor.shape), vmem(2, 2, 12, 16, 128),
             pltpu.VMEM((2, 3, 12, 16, 128), jnp.bfloat16), vmem(128, 128), vmem(128, 128),
             pltpu.VMEM((2, 3, NV, 16, 128), jnp.bfloat16), vmem(3, 8, 128), vmem(3, 6, 8, 128),

time: 31.5 us -> 30.4 us (0.965)
  Pallas kernels: 29.2 us -> 28.1 us
    pallas_call x1, Pallas kernels: 29.2 us -> 28.1 us  [per_device(): pl.pallas_call(kernel, out_shape=(spinor, spinor), in_specs=[anywhere] *...]
where the time goes in v3:
time: 30.4 us; the launch traced here: 30.3 us
  Pallas kernels  28.1 us (92%)
  local copies, waits for them, and re-layouts  1.49 us (5%)
  between operations  0.64 us (2%)
    pallas_call x1, Pallas kernels, per_device(): pl.pallas_call(kernel, out_shape=(spinor, spinor), in_specs=[anywhere] *...  28.1 us
    unnamed x2, local copies, waits for them, and re-layouts  1.49 us

profile of v3, /device:TPU:1, one launch (start us, length us, event | category | flops | bytes accessed | tf_op | source)
XLA Modules:
  0.0 30.3 jit_solution(10551709050964378132)
XLA Ops:
  0.6 28.1 %shard_map.95 = (f32[2,4,3,4,8,128]{5,4,3,2,1,0:T(8,128)S(1)}, f32[2,4,3,4,8,128]{5,4,3,2,1,0:T(8,128)S(1)}) custom-call(f32[2,4,3,4,8,128]{5,4,3,2,1,0:T(8,128)} %source_h.1, f32[2,4,3,4,8,128]{5,4,3,2,1,0:T(8,128)} %iterate_h.1, f32[4,2,3,3,4,8,128]{6,5,4,3,2,1,0:T(8,128)} %links_h.1, f32[2,2,6,6,4,8,128]{6,5,4,3,2,1,0:T(8,128)} %clover_h.1, ...), custom_call_target="tpu_custom_call" | custom-call | tf_op jit(solution)/shard_map/pallas_call | solution.py:509
  28.8 0.7 %copy.13 = f32[2,4,3,4,8,128]{5,4,3,2,1,0:T(8,128)} copy(f32[2,4,3,4,8,128]{5,4,3,2,1,0:T(8,128)S(1)} %get-tuple-element.2) | data formatting | bytes 786432
  29.5 0.7 %copy.14 = f32[2,4,3,4,8,128]{5,4,3,2,1,0:T(8,128)} copy(f32[2,4,3,4,8,128]{5,4,3,2,1,0:T(8,128)S(1)} %get-tuple-element.3) | data formatting | bytes 786432

commit v4 on v3

--- a/solution.py
+++ b/solution.py
@@ -126,13 +126,13 @@
     loads = [
         pltpu.make_async_copy(source_from, into, local_sem.at[i])
         for i, (source_from, into) in enumerate((
-            (iterate_h, iterate), (links_h.at[0:3], links.at[0:3]), (clover_h, clover), (source_h, source),
+            (iterate_h, iterate), (links_h.at[0], links.at[0]), (clover_h, clover), (source_h, source),
             (coarse_h, coarse_b), (null_h, null_b), (links_h.at[3], links.at[3]),
-            (bc_h, bc_ref), (slot_h, slot_ref),
+            (bc_h, bc_ref), (slot_h, slot_ref), (links_h.at[2], links.at[2]), (links_h.at[1], links.at[1]),
         ))
     ]
-    loads[0].start()
-    loads[1].start()
+    for i in (0, 1, 9, 10):
+        loads[i].start()
     barrier = pltpu.get_barrier_semaphore()
     for axis in range(3):
         for step in (-1, 1):
@@ -205,9 +205,15 @@
             pl.semaphore_wait(barrier, 6)
         copies[0].start()
         copies[1].start()
+        if n == 0:
+            loads[9].wait()
+            for i in (7, 8, 6, 2, 3, 5, 4):
+                loads[i].start()
         send_x()
         copies[4].start()
         copies[5].start()
+        if n == 0:
+            loads[10].wait()
         for t in range(4):
             step_z(t, 0)
         copies[2].start()
@@ -314,8 +320,6 @@
 
     loads[0].wait()
     loads[1].wait()
-    for i in (7, 8, 6, 2, 3, 5, 4):
-        loads[i].start()
     first = fine_send(iterate, 0)
     for i in (7, 8, 6, 2):
         loads[i].wait()
@@ -498,6 +502,14 @@
         copy.wait_send()
 
 
+def copy_out(x_v, r_v, x_h, r_h, sem):
+    copies = [pltpu.make_async_copy(x_v, x_h, sem.at[0]), pltpu.make_async_copy(r_v, r_h, sem.at[1])]
+    for copy in copies:
+        copy.start()
+    for copy in copies:
+        copy.wait()
+
+
 def per_device(source, iterate, gauge_links, clover, bc_sign, null_store, block_slot, coarse_links):
     null = null_store.reshape((2, 2, NV, 12, 16, 128))
     coarse = jnp.transpose(coarse_links, (0, 1, 2, 4, 5, 6, 7, 3)).reshape((9, 2, NV, 2, 8, NV))
@@ -506,7 +518,7 @@
     anywhere = pl.BlockSpec(memory_space=pl.ANY)
     half = (2, 2, 3, 8, 128)
     vmem = lambda *shape: pltpu.VMEM(shape, F32)
-    return pl.pallas_call(
+    held = pl.pallas_call(
         kernel,
         out_shape=(spinor, spinor),
         in_specs=[anywhere] * 8,
@@ -522,13 +534,22 @@
             vmem(*spinor.shape), vmem(*spinor.shape), vmem(*spinor.shape), vmem(2, 2, 12, 16, 128),
             pltpu.VMEM((2, 3, 12, 16, 128), jnp.bfloat16), vmem(128, 128), vmem(128, 128),
             pltpu.VMEM((2, 3, NV, 16, 128), jnp.bfloat16), vmem(3, 8, 128), vmem(3, 6, 8, 128),
-            pltpu.SMEM((4,), jnp.int32), pltpu.SMEM((2,), jnp.int32), pltpu.SemaphoreType.DMA((9,)), pltpu.SemaphoreType.DMA((5, 6)),
+            pltpu.SMEM((4,), jnp.int32), pltpu.SMEM((2,), jnp.int32), pltpu.SemaphoreType.DMA((11,)), pltpu.SemaphoreType.DMA((5, 6)),
             pltpu.SemaphoreType.DMA((5, 6)),
         ],
         compiler_params=pltpu.CompilerParams(
             collective_id=0, has_side_effects=True, vmem_limit_bytes=56 * 1024 * 1024
         ),
     )(source, iterate, gauge_links, clover, null, coarse, bc_sign, slots)
+    held = [pltpu.with_memory_space_constraint(x, pltpu.VMEM) for x in held]
+    final = jax.ShapeDtypeStruct(spinor.shape, F32)
+    return pl.pallas_call(
+        copy_out,
+        out_shape=(final, final),
+        in_specs=[pl.BlockSpec(memory_space=pltpu.VMEM)] * 2,
+        out_specs=(anywhere, anywhere),
+        scratch_shapes=[pltpu.SemaphoreType.DMA((2,))],
+    )(*held)
 
 
 def solution(mesh):

time: 30.4 us -> 29.8 us (0.980)
  local copies, waits for them, and re-layouts: 1.49 us -> 0 us
  Pallas kernels: 28.1 us -> 29 us
    unnamed x2 -> x0, local copies, waits for them, and re-layouts: 1.49 us -> none
    pallas_call x0 -> x1, Pallas kernels: none -> 0.89 us  [per_device(): pl.pallas_call(copy_out, out_shape=(final, final), in_specs=[pl.BlockSpec...]
where the time goes in v4:
time: 29.8 us; the launch traced here: 29.6 us
  Pallas kernels  29 us (97%)
  between operations  0.64 us (2%)
    pallas_call x1, Pallas kernels, per_device(): pl.pallas_call(kernel, out_shape=(spinor, spinor), in_specs=[anywhere] *...  28.1 us
    pallas_call x1, Pallas kernels, per_device(): pl.pallas_call(copy_out, out_shape=(final, final), in_specs=[pl.BlockSpec...  0.89 us

profile of v4, /device:TPU:1, one launch (start us, length us, event | category | flops | bytes accessed | tf_op | source)
XLA Modules:
  0.0 29.6 jit_solution(2327517105737631384)
XLA Ops:
  0.6 28.1 %shard_map.95 = (f32[2,4,3,4,8,128]{5,4,3,2,1,0:T(8,128)S(1)}, f32[2,4,3,4,8,128]{5,4,3,2,1,0:T(8,128)S(1)}) custom-call(f32[2,4,3,4,8,128]{5,4,3,2,1,0:T(8,128)} %source_h.1, f32[2,4,3,4,8,128]{5,4,3,2,1,0:T(8,128)} %iterate_h.1, f32[4,2,3,3,4,8,128]{6,5,4,3,2,1,0:T(8,128)} %links_h.1, f32[2,2,6,6,4,8,128]{6,5,4,3,2,1,0:T(8,128)} %clover_h.1, ...), custom_call_target="tpu_custom_call" | custom-call | tf_op jit(solution)/shard_map/pallas_call | solution.py:521
  28.7 0.9 %shard_map.96 = (f32[2,4,3,4,8,128]{5,4,3,2,1,0:T(8,128)}, f32[2,4,3,4,8,128]{5,4,3,2,1,0:T(8,128)}) custom-call(f32[2,4,3,4,8,128]{5,4,3,2,1,0:T(8,128)S(1)} %get-tuple-element.4.x_v, f32[2,4,3,4,8,128]{5,4,3,2,1,0:T(8,128)S(1)} %get-tuple-element.5.r_v), custom_call_target="tpu_custom_call" | custom-call | tf_op jit(solution)/shard_map/pallas_call | solution.py:546

commit v5 on v4

--- a/solution.py
+++ b/solution.py
@@ -360,8 +360,8 @@
         slot = slot_ref[z]
 
         def restrict_step(i, carry):
-            for j in range(4):
-                first_v = 8 * i + 2 * j
+            for j in range(12):
+                first_v = 2 * j
                 totals = [[None, None], [None, None]]
                 for s in range(12):
                     for u in range(2):
@@ -376,7 +376,7 @@
                         rrow[pl.ds(64 * q + 32 * z + first_v + u, 1)] = jnp.sum(totals[u][q], axis=0, keepdims=True)
             return carry
 
-        lax.fori_loop(0, NV // 8, restrict_step, 0)
+        restrict_step(0, 0)
 
     rhs = lax.dot_general(
         spread, rrow[...], (((1,), (1,)), ((), ())), precision=HIGHEST, preferred_element_type=F32
@@ -475,7 +475,7 @@
                             totals[u][q] = running(totals[u][q], null, tile[z, kind, v])
             for u in range(2):
                 s = 2 * i + u
-                spin, colour = s // 3, lax.rem(s, 3)
+                spin, colour = s // 3, s % 3
                 for q in range(2):
                     for t in range(4):
                         corr[q, spin, colour, t, 4 * z : 4 * z + 4] = totals[u][q][4 * t : 4 * t + 4]
@@ -485,7 +485,8 @@
             prolong_step(2 * i, carry)
             return prolong_step(2 * i + 1, carry)
 
-        lax.fori_loop(0, 3, prolong_pair, 0)
+        for i in range(3):
+            prolong_pair(i, 0)
 
     second = fine_send(corr, 1)
 

time: 29.8 us -> 29.7 us (level)
  no operation moved by 1% of the time
where the time goes in v5:
time: 29.7 us; the launch traced here: 29.5 us
  Pallas kernels  28.9 us (97%)
  between operations  0.64 us (2%)
    pallas_call x1, Pallas kernels, per_device(): pl.pallas_call(kernel, out_shape=(spinor, spinor), in_specs=[anywhere] *...  28 us
    pallas_call x1, Pallas kernels, per_device(): pl.pallas_call(copy_out, out_shape=(final, final), in_specs=[pl.BlockSpec...  0.89 us

profile of v5, /device:TPU:1, one launch (start us, length us, event | category | flops | bytes accessed | tf_op | source)
XLA Modules:
  0.0 29.5 jit_solution(1207957980749765368)
XLA Ops:
  0.6 28.0 %shard_map.95 = (f32[2,4,3,4,8,128]{5,4,3,2,1,0:T(8,128)S(1)}, f32[2,4,3,4,8,128]{5,4,3,2,1,0:T(8,128)S(1)}) custom-call(f32[2,4,3,4,8,128]{5,4,3,2,1,0:T(8,128)} %source_h.1, f32[2,4,3,4,8,128]{5,4,3,2,1,0:T(8,128)} %iterate_h.1, f32[4,2,3,3,4,8,128]{6,5,4,3,2,1,0:T(8,128)} %links_h.1, f32[2,2,6,6,4,8,128]{6,5,4,3,2,1,0:T(8,128)} %clover_h.1, ...), custom_call_target="tpu_custom_call" | custom-call | tf_op jit(solution)/shard_map/pallas_call | solution.py:522
  28.6 0.9 %shard_map.96 = (f32[2,4,3,4,8,128]{5,4,3,2,1,0:T(8,128)}, f32[2,4,3,4,8,128]{5,4,3,2,1,0:T(8,128)}) custom-call(f32[2,4,3,4,8,128]{5,4,3,2,1,0:T(8,128)S(1)} %get-tuple-element.4.x_v, f32[2,4,3,4,8,128]{5,4,3,2,1,0:T(8,128)S(1)} %get-tuple-element.5.r_v), custom_call_target="tpu_custom_call" | custom-call | tf_op jit(solution)/shard_map/pallas_call | solution.py:547
